TPU v7x, 32 devices: a whole 2x2x4 slice. The times are simulated.
32 devices in a mesh: expert: 4 (over x, core), ffn: 8 (over z, y).
Axes of the slice: x: 2, y: 2, z: 4, core: 2. Of those that a mesh axis runs over, the one named last changes fastest.
Arguments:
- tokens: bfloat16 [4, 32, 4096], P('expert', 'ffn'), may hold values from -6 to 6
- routes: int32 [4, 32, 2], P('expert'), may hold values from 0 to 3, all different within a row; in each aligned block of 32 rows (0 to 31, 32 to 63, ..., all dimensions but the last counted through in order) at most 24 rows name the same one
- router: bfloat16 [4096, 4], replicated, may hold values from -0.09375 to 0.09375
- w_gate: bfloat16 [4, 4096, 12288], P('expert', None, 'ffn'), may hold values from -0.09375 to 0.09375
- w_up: bfloat16 [4, 4096, 12288], P('expert', None, 'ffn'), may hold values from -0.09375 to 0.09375
- w_down: bfloat16 [4, 12288, 4096], P('expert', 'ffn'), may hold values from -0.078125 to 0.078125
- adapter: bfloat16 [4, 4096, 4096], P('expert', None, 'ffn'), may hold values from -0.09375 to 0.09375
- upstream: bfloat16 [4, 32, 4096], P('expert', None, 'ffn'), may hold values from -24 to 24
- bound: float32 [4], P('expert'), may hold values from 2048 to 16384
Outputs:
- adapted: bfloat16 [4, 32, 4096], P('expert', None, 'ffn')
- clipped: bfloat16 [4, 4096, 4096], P('expert', None, 'ffn')
Inputs may be any that keep to these rules, and one draw needn't show every extreme that they name: `routes`: each token names two different experts; for each client at most 24 of its tokens name any one expert, and in some clients some expert is named by exactly 24 tokens.
All inputs are finite; a program needn't handle non-finite values.
Results may differ from a plain program's by a relative error of at most 0.015.
Values may be sent and summed in bfloat16 or wider, within the bound.
A program may use at most 128 MiB of HBM per device.

v0:
```python
import jax
import jax.numpy as jnp
from jax import lax
from jax.sharding import PartitionSpec as P


def slot_table(routed, expert_count):
    named_hits = jnp.sum(
        (routed[:, :, None] == jnp.arange(expert_count, dtype=jnp.int32)[None, None, :]).astype(
            jnp.int32
        ),
        axis=1,
    )
    before = jnp.cumsum(named_hits, axis=0) - named_hits
    return jnp.take_along_axis(before, routed, axis=1)


def pack_rows(token_rows, routed, expert_count, capacity):
    token_count = token_rows.shape[0]
    slot_flat = routed * capacity + slot_table(routed, expert_count)
    owners = jnp.repeat(jnp.arange(token_count, dtype=jnp.int32), 2)
    source = (
        jnp.full((expert_count * capacity,), token_count, jnp.int32)
        .at[slot_flat.reshape(-1)]
        .set(owners)
    )
    padded = jnp.concatenate(
        [token_rows, jnp.zeros((1, token_rows.shape[1]), token_rows.dtype)], axis=0
    )
    return (padded[source].reshape(expert_count, capacity, token_rows.shape[1]), slot_flat)


def mix_weights(token_rows, routed, router):
    logits = jnp.dot(token_rows, router, preferred_element_type=jnp.float32)
    picked = jnp.take_along_axis(logits, routed, axis=1)
    weight_first = jax.nn.sigmoid(picked[:, 0] - picked[:, 1])
    return (weight_first, 1.0 - weight_first)


def per_device(tokens, routes, router, w_gate, w_up, w_down, adapter, upstream, bound):
    expert_count = lax.axis_size("expert")
    gathered = lax.all_gather(tokens, "ffn", axis=1, tiled=True)
    token_rows = gathered[0]
    token_count = token_rows.shape[0]
    model_width = token_rows.shape[1]
    capacity = 3 * token_count // expert_count
    routed = routes[0]
    outgoing, slot_flat = pack_rows(token_rows, routed, expert_count, capacity)
    col_count = adapter.shape[2]
    column = lax.axis_index("ffn") * col_count
    weight_first, weight_second = mix_weights(token_rows, routed, router)
    arrived = lax.all_to_all(outgoing, "expert", split_axis=0, concat_axis=0, tiled=True)
    flat_rows = arrived.reshape(-1, model_width)
    gate_out = jnp.dot(flat_rows, w_gate[0], preferred_element_type=jnp.float32)
    up_out = jnp.dot(flat_rows, w_up[0], preferred_element_type=jnp.float32)
    hidden = (jax.nn.silu(gate_out) * up_out).astype(jnp.bfloat16)
    down_piece = jnp.dot(hidden, w_down[0], preferred_element_type=jnp.float32).astype(jnp.bfloat16)
    returned = lax.all_to_all(
        down_piece.reshape(arrived.shape), "expert", split_axis=0, concat_axis=0, tiled=True
    )
    picked = returned.reshape(-1, model_width)[slot_flat]
    mix_share = weight_first[:, None] * picked[:, 0].astype(jnp.float32) + weight_second[
        :, None
    ] * picked[:, 1].astype(jnp.float32)
    mixture = lax.psum(mix_share, "ffn")
    layer_out = (token_rows.astype(jnp.float32) + mixture).astype(jnp.bfloat16)
    own_cols = lax.dynamic_slice_in_dim(layer_out, column, col_count, 1)
    adapted = (
        own_cols.astype(jnp.float32)
        + jnp.dot(layer_out, adapter[0], preferred_element_type=jnp.float32)
    ).astype(jnp.bfloat16)
    grad_input = upstream[0]
    adapter_grad = lax.dot_general(
        layer_out, grad_input, (((0,), (0,)), ((), ())), preferred_element_type=jnp.float32
    )
    cotangent_gram = lax.dot_general(
        grad_input, grad_input, (((1,), (1,)), ((), ())), preferred_element_type=jnp.float32
    )
    whole_gram = lax.psum(cotangent_gram, "ffn")
    layer_gram = lax.dot_general(
        layer_out, layer_out, (((1,), (1,)), ((), ())), preferred_element_type=jnp.float32
    )
    squared = jnp.sum(layer_gram * whole_gram)
    grad_norm = jnp.sqrt(squared)
    clip_limit = bound[0]
    factor = clip_limit / jnp.maximum(grad_norm, clip_limit)
    clipped = (adapter_grad * factor).astype(jnp.bfloat16)
    return (adapted[None], clipped[None])


def solution(mesh):
    in_specs = (
        P("expert", "ffn", None),
        P("expert", None, None),
        P(),
        P("expert", None, "ffn"),
        P("expert", None, "ffn"),
        P("expert", "ffn", None),
        P("expert", None, "ffn"),
        P("expert", None, "ffn"),
        P("expert"),
    )
    out_specs = (P("expert", None, "ffn"), P("expert", None, "ffn"))
    return jax.shard_map(
        per_device, mesh=mesh, in_specs=in_specs, out_specs=out_specs, check_vma=False
    )
```

profile of v0, /device:TPU:0, one launch (start us, length us, event | category | flops | bytes accessed | tf_op | source)
XLA Modules:
  0.0 190.7 jit_solution(15884546444229429780)
XLA Ops:
  7.2 0.0 copy-start
  7.2 0.0 copy-start.1
  7.2 0.7 shift-left_or_fusion
  7.9 0.8 copy.46
  8.6 0.7 convert_reduce_fusion
  9.3 0.1 copy.47
  9.4 0.1 copy.44
  9.5 0.1 reshape.206
  9.6 0.1 reduce_window_sum.11
  9.7 0.1 squeeze.35
  9.8 0.1 reshape.222
  9.9 0.0 copy-start.3
  9.9 0.8 gather_fusion.3
  10.7 0.8 scatter_custom_fusion
  11.5 0.0 copy-done.1
  11.6 0.1 copy.43
  11.6 33.0 %all_gather.3 = bf16[1,32,4096]{2,0,1:T(2,128)(2,1)S(1)} all-gather(bf16[1,4,4096]{2,0,1:T(2,128)(2,1)S(1)} %copy.43), channel_id=1, replica_groups=mesh['expert'=4,'ffn'=8] {'ffn'}, dimensions={1}, use_global_device_ids=true | all-gather | bytes 294912 | tf_op jit(solution)/shard_map/all_gather | solution.py:42
  44.6 0.3 copy.65
  45.0 1.9 %gather_fusion = bf16[96,4096]{1,0:T(8,128)(2,1)} fusion(bf16[33,4096]{1,0:T(8,128)(2,1)S(1)} %concatenate.3, s32[1024]{0:T(1024)S(1)} %pad_clamp_fusion.1), kind=kCustom, calls=%fused_computation | custom fusion | bytes 1573248 | tf_op jit(solution)/shard_map/gather | solution.py:30
  46.9 3.5 %all-to-all-start = ((bf16[4,24,4096]{2,1,0:T(8,128)(2,1)}), bf16[4,24,4096]{2,1,0:T(8,128)(2,1)S(1)}, u32[]{:S(2)}, u32[]{:S(2)}) async-start(bf16[4,24,4096]{2,1,0:T(8,128)(2,1)} %bitcast.5), calls=%async_computation | async-start | bytes 1572864 | tf_op jit(solution)/shard_map/all_to_all | solution.py:52
  50.4 0.1 gather.22
  50.5 0.1 copy.49
  50.6 0.0 copy-done.3
  50.6 0.2 fusion.43
  50.8 11.2 %all-to-all-done = bf16[4,24,4096]{2,1,0:T(8,128)(2,1)S(1)} async-done(((bf16[4,24,4096]{2,1,0:T(8,128)(2,1)}), bf16[4,24,4096]{2,1,0:T(8,128)(2,1)S(1)}, u32[]{:S(2)}, u32[]{:S(2)}) %all-to-all-start) | async-done | bytes 786464 | tf_op jit(solution)/shard_map/all_to_all | solution.py:52
  62.0 6.7 %fusion.4 = f32[96,1536]{1,0:T(8,128)S(1)} fusion(bf16[96,4096]{1,0:T(8,128)(2,1)S(1)} %bitcast.93, bf16[1,4096,1536]{2,1,0:T(8,128)(2,1)} %param.12), kind=kOutput, calls=%fused_computation.9 | convolution fusion | flops 1207959552 | bytes 13959168 | tf_op jit(solution)/shard_map/dot_general | solution.py:54
  68.6 0.0 copy-start.2
  68.7 13.3 %fusion.7 = bf16[96,4096]{1,0:T(8,128)(2,1)} fusion(bf16[1,1536,4096]{2,1,0:T(8,128)(2,1)} %param.14, bf16[96,4096]{1,0:T(8,128)(2,1)S(1)} %bitcast.94, bf16[1,4096,1536]{2,1,0:T(8,128)(2,1)} %param.13, f32[96,1536]{1,0:T(8,128)S(1)} %fusion.4), kind=kOutput, calls=%fused_computation.13 | convolution fusion | flops 2417197056 | bytes 27328512 | tf_op jit(solution)/shard_map/dot_general | solution.py:57
  82.0 3.5 %all-to-all-start.1 = ((bf16[4,24,4096]{2,1,0:T(8,128)(2,1)}), bf16[4,24,4096]{2,1,0:T(8,128)(2,1)S(1)}, u32[]{:S(2)}, u32[]{:S(2)}) async-start(bf16[4,24,4096]{2,1,0:T(8,128)(2,1)} %bitcast.10), calls=%async_computation.1 | async-start | bytes 1572864 | tf_op jit(solution)/shard_map/all_to_all | solution.py:58
  85.5 0.0 all-reduce.3.cloned.1.call-start
  85.5 0.0 copy-done.2
  85.5 0.1 copy.50
  85.6 0.1 reshape.200
  85.7 0.9 gather_fusion.2
  86.6 0.1 reshape.209
  86.7 0.1 copy.45
  86.8 10.2 %all-to-all-done.1 = bf16[4,24,4096]{2,1,0:T(8,128)(2,1)S(1)} async-done(((bf16[4,24,4096]{2,1,0:T(8,128)(2,1)}), bf16[4,24,4096]{2,1,0:T(8,128)(2,1)S(1)}, u32[]{:S(2)}, u32[]{:S(2)}) %all-to-all-start.1) | async-done | bytes 786464 | tf_op jit(solution)/shard_map/all_to_all | solution.py:58
  97.0 0.9 gather_fusion.1
  97.9 0.3 reshape.199
  98.3 1.2 fusion.42
  99.4 1.4 fusion.31
  100.9 0.0 all-reduce.3.cloned.1.call-update
  101.6 0.0 copy-done
  101.6 0.1 fusion.33
  101.7 37.4 %psum.15 = f32[32,32]{1,0:T(8,128)S(1)} all-reduce(f32[32,32]{1,0:T(8,128)S(1)} %fusion.33), channel_id=1, replica_groups=mesh['expert'=4,'ffn'=8] {'ffn'}, use_global_device_ids=true, to_apply=%region_4.5 | all-reduce | flops 1024 | bytes 8192 | tf_op jit(solution)/shard_map/psum | solution.py:79
  139.1 35.0 %all-reduce.3.cloned.1.call-done = f32[32,4096]{1,0:T(8,128)} async-done(((f32[32,4096]{1,0:T(8,128)}), f32[32,4096]{1,0:T(8,128)}) %all-reduce.3.cloned.1.call-update) | async-done | bytes 524304 | tf_op jit(solution)/shard_map/psum | solution.py:65
  174.1 1.4 add_convert_fusion
  175.4 0.8 fusion.30
  177.0 3.3 %fusion.6 = bf16[1,4096,512]{2,1,0:T(8,128)(2,1)} fusion(bf16[32,4096]{1,0:T(8,128)(2,1)S(1)} %add_convert_fusion, f32[]{:T(128)S(6)} %div.14, bf16[1,32,512]{2,1,0:T(8,128)(2,1)S(1)} %copy-done), kind=kOutput, calls=%fused_computation.12 | convolution fusion | flops 138412032 | bytes 4489220 | tf_op jit(solution)/shard_map/dot_general | solution.py:73
  180.2 3.6 %fusion.24 = bf16[1,32,512]{2,1,0:T(8,128)(2,1)} fusion(bf16[32,4096]{1,0:T(8,128)(2,1)S(1)} %add_convert_fusion, bf16[1,4096,512]{2,1,0:T(8,128)(2,1)} %param.15, s32[]{:T(128)S(6)} %select_n.91), kind=kOutput, calls=%fused_computation.20 | convolution fusion | flops 134266880 | bytes 4521988 | tf_op jit(solution)/shard_map/dot_general | solution.py:70
  (10 shorter events, 0.1 us)
Async XLA Ops:
  7.2 94.4 %copy-start = (bf16[1,32,512]{2,1,0:T(8,128)(2,1)S(1)}, bf16[1,32,512]{2,1,0:T(8,128)(2,1)}, u32[]{:S(2)}) copy-start(bf16[1,32,512]{2,1,0:T(8,128)(2,1)} %param.16) | copy-start | bytes 98308
  7.2 4.4 %copy-start.1 = (bf16[1,4,4096]{2,1,0:T(4,128)(2,1)S(1)}, bf16[1,4,4096]{2,1,0:T(4,128)(2,1)}, u32[]{:S(2)}) copy-start(bf16[1,4,4096]{2,1,0:T(4,128)(2,1)} %param.9) | copy-start | bytes 98308
  9.9 40.7 %copy-start.3 = (bf16[4096,4]{0,1:T(4,128)(2,1)S(1)}, bf16[4096,4]{0,1:T(4,128)(2,1)}, u32[]{:S(2)}) copy-start(bf16[4096,4]{0,1:T(4,128)(2,1)} %param.11) | copy-start | bytes 98308
  46.9 15.1 %all-to-all-start = ((bf16[4,24,4096]{2,1,0:T(8,128)(2,1)}), bf16[4,24,4096]{2,1,0:T(8,128)(2,1)S(1)}, u32[]{:S(2)}, u32[]{:S(2)}) async-start(bf16[4,24,4096]{2,1,0:T(8,128)(2,1)} %bitcast.5), calls=%async_computation | async-start | bytes 1572864 | tf_op jit(solution)/shard_map/all_to_all | solution.py:52
  68.6 16.9 %copy-start.2 = (s32[1,32,2]{1,2,0:T(2,128)S(1)}, s32[1,32,2]{1,2,0:T(2,128)}, u32[]{:S(2)}) copy-start(s32[1,32,2]{1,2,0:T(2,128)} %param.10) | copy-start | bytes 772
  82.0 15.1 %all-to-all-start.1 = ((bf16[4,24,4096]{2,1,0:T(8,128)(2,1)}), bf16[4,24,4096]{2,1,0:T(8,128)(2,1)S(1)}, u32[]{:S(2)}, u32[]{:S(2)}) async-start(bf16[4,24,4096]{2,1,0:T(8,128)(2,1)} %bitcast.10), calls=%async_computation.1 | async-start | bytes 1572864 | tf_op jit(solution)/shard_map/all_to_all | solution.py:58
  85.5 88.6 %all-reduce.3.cloned.1.call-start = ((), (), s32[]{:S(2)}) async-start(), calls=%async_computation.2 | async-start | bytes 1048576 | tf_op jit(solution)/shard_map/psum | solution.py:65
Sparse Core Ops, SparseCore 0:
  101.0 72.9 all-reduce.2
where the time goes:
time: 191 us
  blocking collectives  70.4 us (37%)
  waiting for transfers between devices  56.4 us (30%)
  matrix products  28 us (15%)
  between operations  15.6 us (8%)
  local copies, waits for them, and re-layouts  8.92 us (5%)
  starting transfers between devices  7.03 us (4%)
  other arithmetic  4.31 us (2%)
    psum x1, blocking collectives, per_device(): whole_gram = lax.psum(cotangent_gram, 'ffn')  37.4 us
    psum x1, waiting for transfers between devices, per_device(): mixture = lax.psum(mix_share, 'ffn')  35 us
    all_gather x1, blocking collectives, per_device(): gathered = lax.all_gather(tokens, 'ffn', axis=1, tiled=True)  33 us
    dot_general x1, matrix products, per_device(): jnp.dot(hidden, w_down[0], preferred_element_type=jnp.float32)  13.3 us
    all_to_all x1, waiting for transfers between devices, per_device(): lax.all_to_all(outgoing, 'expert', split_axis=0, concat_axis=0, tiled=True)  11.2 us
    all_to_all x1, waiting for transfers between devices, per_device(): lax.all_to_all(down_piece.reshape(arrived.shape), 'expert', split_axis=0,...  10.2 us
    dot_general x1, matrix products, per_device(): gate_out = jnp.dot(flat_rows, w_gate[0], preferred_element_type=jnp.float32)  6.66 us
  transfers between devices with their start and end apart: 3, of which 3 were waited for; matrix products, arithmetic and copies ran while one was open for 1% of the time, Pallas kernels for 0%

commit v1 on v0

v1 whole, which is shorter than its diff:
```python
import functools

import jax
import jax.numpy as jnp
from jax import lax
from jax.experimental import pallas as pl
from jax.experimental.pallas import tpu as pltpu
from jax.sharding import PartitionSpec as P

MESH = pl.DeviceIdType.MESH
CORES = 2


def tile_of(size, choices=(512, 384, 256, 128)):
    for width in choices:
        if size % width == 0:
            return width
    return size


def layer_kernel(
    dims,
    tok_ref, routes_ref, router_ref, wg_hbm, wu_hbm, wd_hbm, ad_hbm, up_ref, bound_ref,
    layer_ref, adapted_ref, factor_ref,
    wg, wu, wd, ad, tokbuf, tokc, gate_acc, up_acc, hid, logit_acc, routes_buf, gram_buf,
    sbuf, r1, s2, r2, s3, r3, lbuf,
    w_sem, own_sem, rt_send, rt_recv, gr_send, gr_recv, tf_send, tf_recv, tx_send, tx_recv,
    tc_send, tc_recv, a_send, a_recv, b_send, b_recv, c_send, c_recv, d_send, d_recv,
):
    E, F, KC, NC, D, FFD, t, tl, cd = dims
    X = E // CORES
    T = E * t
    KW = D // KC
    NW = D // NC
    CW = NW // F
    e = lax.axis_index("expert")
    f = lax.axis_index("ffn")
    x, core = e // CORES, lax.rem(e, CORES)
    mate = x * CORES + (CORES - 1 - core)

    loads = {}
    for k in range(KC):
        loads["g", k] = pltpu.make_async_copy(
            wg_hbm.at[pl.ds(k * KW, KW), :], wg.at[k], w_sem.at[0, k]
        )
        loads["u", k] = pltpu.make_async_copy(
            wu_hbm.at[pl.ds(k * KW, KW), :], wu.at[k], w_sem.at[1, k]
        )
    for j in range(NC):
        loads["d", j] = pltpu.make_async_copy(
            wd_hbm.at[:, pl.ds(j * NW, NW)], wd.at[j], w_sem.at[2, j]
        )
    loads["a", 0] = pltpu.make_async_copy(ad_hbm, ad, w_sem.at[3, 0])
    for load in loads.values():
        load.start()
    own = []
    for k in range(KC):
        copy = pltpu.make_async_copy(
            tok_ref.at[:, pl.ds(k * KW, KW)], tokbuf.at[k, e, f], own_sem.at[k]
        )
        copy.start()
        own.append(copy)
    own_routes = pltpu.make_async_copy(routes_ref, routes_buf.at[e], own_sem.at[KC])
    own_routes.start()
    gram_buf[f] = lax.dot_general(
        up_ref[...], up_ref[...], (((1,), (1,)), ((), ())), preferred_element_type=jnp.float32
    )

    barrier = pltpu.get_barrier_semaphore()
    for d in range(1, F):
        pl.semaphore_signal(
            barrier, inc=1, device_id={"ffn": lax.rem(f + d, F)}, device_id_type=MESH
        )
    for d in range(1, E):
        pl.semaphore_signal(
            barrier, inc=1, device_id={"expert": lax.rem(e + d, E)}, device_id_type=MESH
        )
    pl.semaphore_wait(barrier, F + E - 2)

    sent = []

    def send(src, dst, send_sem, recv_sem, device):
        copy = pltpu.make_async_remote_copy(
            src_ref=src, dst_ref=dst, send_sem=send_sem, recv_sem=recv_sem,
            device_id=device, device_id_type=MESH,
        )
        copy.start()
        sent.append(copy)

    def receive(dst, send_sem, recv_sem, device):
        pltpu.make_async_remote_copy(
            src_ref=dst, dst_ref=dst, send_sem=send_sem, recv_sem=recv_sem,
            device_id=device, device_id_type=MESH,
        ).wait_recv()

    def ffn_to(d):
        return {"ffn": lax.rem(f + d, F)}

    def ffn_from(d):
        return lax.rem(f + F - d, F)

    def x_to(d):
        return lax.rem(x + d, X)

    def x_from(d):
        return lax.rem(x + X - d, X)

    for k in range(KC):
        for d in range(1, F):
            send(
                tok_ref.at[:, pl.ds(k * KW, KW)], tokbuf.at[k, e, f],
                tf_send.at[k, d], tf_recv.at[k, d], ffn_to(d),
            )
    for d in range(1, E):
        send(
            routes_ref, routes_buf.at[e], rt_send.at[d], rt_recv.at[d],
            {"expert": lax.rem(e + d, E)},
        )
    for d in range(1, F):
        send(gram_buf.at[f], gram_buf.at[f], gr_send.at[d], gr_recv.at[d], ffn_to(d))

    def forward_client(k):
        own[k].wait()
        for d in range(1, F):
            receive(
                tokbuf.at[k, e, ffn_from(d)], tf_send.at[k, d], tf_recv.at[k, d], ffn_to(d)
            )
        for d in range(1, X):
            send(
                tokbuf.at[k, e], tokbuf.at[k, e], tx_send.at[k, d], tx_recv.at[k, d],
                {"expert": x_to(d) * CORES + core},
            )
        send(
            tokbuf.at[k, e], tokbuf.at[k, e], tc_send.at[k, 0], tc_recv.at[k, 0],
            {"expert": mate},
        )

    def forward_x(k):
        for d in range(1, X):
            block = x_from(d) * CORES + core
            receive(
                tokbuf.at[k, block], tx_send.at[k, d], tx_recv.at[k, d], {"expert": block}
            )
            send(
                tokbuf.at[k, block], tokbuf.at[k, block], tc_send.at[k, d], tc_recv.at[k, d],
                {"expert": mate},
            )

    FT = tile_of(FFD)

    def expand(k):
        for d in range(X):
            block = x_from(d) * CORES + (CORES - 1 - core)
            receive(
                tokbuf.at[k, block], tc_send.at[k, d], tc_recv.at[k, d], {"expert": mate}
            )

        def compact(c, carry):
            rows = jnp.concatenate(
                [tokbuf[k, c, i].astype(jnp.float32) for i in range(F)], axis=0
            ).astype(jnp.bfloat16)
            tokc[k, pl.ds(pl.multiple_of(c * t, t), t), :] = rows
            return carry

        lax.fori_loop(0, E, compact, 0)
        loads["g", k].wait()
        loads["u", k].wait()

        def hidden_tile(i, carry):
            cols = pl.ds(pl.multiple_of(i * FT, FT), FT)
            g = jnp.dot(tokc[k], wg[k, :, cols], preferred_element_type=jnp.float32)
            u = jnp.dot(tokc[k], wu[k, :, cols], preferred_element_type=jnp.float32)
            if k > 0:
                g = gate_acc[:, cols] + g
                u = up_acc[:, cols] + u
            if k < KC - 1:
                gate_acc[:, cols] = g
                up_acc[:, cols] = u
            else:
                hid[:, cols] = (g / (1.0 + jnp.exp(-g)) * u).astype(jnp.bfloat16)
            return carry

        lax.fori_loop(0, FFD // FT, hidden_tile, 0)
        part = jnp.dot(
            tokc[k], router_ref[pl.ds(k * KW, KW), :], preferred_element_type=jnp.float32
        )
        logit_acc[...] = part if k == 0 else logit_acc[...] + part

    for step in range(KC + 2):
        if step < KC:
            forward_client(step)
        if 0 <= step - 1 < KC:
            forward_x(step - 1)
        if 0 <= step - 2:
            expand(step - 2)

    own_routes.wait()
    for d in range(1, E):
        receive(
            routes_buf.at[lax.rem(e + E - d, E)], rt_send.at[d], rt_recv.at[d],
            {"expert": lax.rem(e + d, E)},
        )
    routed = routes_buf[...].reshape(T, 2)
    logits = logit_acc[...]
    expert_ids = lax.broadcasted_iota(jnp.int32, (T, E), 1)
    first, second = routed[:, 0:1], routed[:, 1:2]
    picked_first = jnp.sum(jnp.where(expert_ids == first, logits, 0.0), axis=1, keepdims=True)
    picked_second = jnp.sum(jnp.where(expert_ids == second, logits, 0.0), axis=1, keepdims=True)
    weight_first = 1.0 / (1.0 + jnp.exp(picked_second - picked_first))
    share = jnp.where(first == e, weight_first, 0.0) + jnp.where(
        second == e, 1.0 - weight_first, 0.0
    )

    NT = tile_of(NW, (256, 128))

    def down(j):
        loads["d", j].wait()
        for n in range(NW // NT):
            value = jnp.dot(
                hid[...], wd[j, :, n * NT:(n + 1) * NT], preferred_element_type=jnp.float32
            )
            value = (value * share).astype(jnp.bfloat16)
            for c in range(E):
                for q in range(NT // CW):
                    sbuf[j, c % CORES, c // CORES, n * (NT // CW) + q] = value[
                        c * t:(c + 1) * t, q * CW:(q + 1) * CW
                    ]
        send(
            sbuf.at[j, CORES - 1 - core], r1.at[j], a_send.at[j], a_recv.at[j],
            {"expert": mate},
        )

    def add_mate(j):
        receive(r1.at[j], a_send.at[j], a_recv.at[j], {"expert": mate})
        for d in range(1, X + 1):
            to = x_to(d)
            s2[j, to] = (
                sbuf[j, core, to].astype(jnp.float32) + r1[j, to].astype(jnp.float32)
            ).astype(jnp.bfloat16)
            if d < X:
                send(
                    s2.at[j, to], r2.at[j, d], b_send.at[j, d], b_recv.at[j, d],
                    {"expert": to * CORES + core},
                )

    def add_x(j):
        total = s2[j, x].astype(jnp.float32)
        for d in range(1, X):
            receive(
                r2.at[j, d], b_send.at[j, d], b_recv.at[j, d],
                {"expert": x_from(d) * CORES + core},
            )
            total = total + r2[j, d].astype(jnp.float32)
        s3[j] = total.astype(jnp.bfloat16)
        for d in range(1, F):
            send(
                s3.at[j, lax.rem(f + d, F)], r3.at[j, d], c_send.at[j, d], c_recv.at[j, d],
                ffn_to(d),
            )

    def add_ffn(j):
        total = s3[j, f].astype(jnp.float32)
        for d in range(1, F):
            receive(r3.at[j, d], c_send.at[j, d], c_recv.at[j, d], ffn_to(d))
            total = total + r3[j, d].astype(jnp.float32)
        start = j * NW
        column = pl.multiple_of(lax.rem(start, KW) + f * CW, CW)
        rows = pl.ds(pl.multiple_of(e * t, t), t)
        if NW <= KW:
            mine = tokc[start // KW, rows, pl.ds(column, CW)]
        else:
            place = start + f * CW
            mine = tokc[place // KW, rows, pl.ds(pl.multiple_of(lax.rem(place, KW), CW), CW)]
        lbuf[j, f] = (mine.astype(jnp.float32) + total).astype(jnp.bfloat16)
        for d in range(1, F):
            send(lbuf.at[j, f], lbuf.at[j, f], d_send.at[j, d], d_recv.at[j, d], ffn_to(d))

    for step in range(NC + 5):
        if step < NC:
            down(step)
        if 0 <= step - 1 < NC:
            add_mate(step - 1)
        if 0 <= step - 3 < NC:
            add_x(step - 3)
        if 0 <= step - 5 < NC:
            add_ffn(step - 5)

    for d in range(1, F):
        receive(gram_buf.at[ffn_from(d)], gr_send.at[d], gr_recv.at[d], ffn_to(d))
    whole_gram = jnp.sum(gram_buf[...], axis=0)
    loads["a", 0].wait()
    layer_gram = jnp.zeros((t, t), jnp.float32)
    adapted = jnp.zeros((t, cd), jnp.float32)
    for j in range(NC):
        for d in range(1, F):
            receive(lbuf.at[j, ffn_from(d)], d_send.at[j, d], d_recv.at[j, d], ffn_to(d))
        block = jnp.concatenate([lbuf[j, i] for i in range(F)], axis=1)
        layer_ref[:, j * NW:(j + 1) * NW] = block
        layer_gram = layer_gram + lax.dot_general(
            block, block, (((1,), (1,)), ((), ())), preferred_element_type=jnp.float32
        )
        adapted = adapted + jnp.dot(
            block, ad[j * NW:(j + 1) * NW, :], preferred_element_type=jnp.float32
        )
    own_cols = layer_ref[:, pl.ds(pl.multiple_of(f * cd, cd), cd)]
    adapted_ref[...] = (own_cols.astype(jnp.float32) + adapted).astype(jnp.bfloat16)
    squared = jnp.sum(
        jnp.sum(layer_gram * whole_gram, axis=1, keepdims=True), axis=0, keepdims=True
    )
    limit = bound_ref[0]
    norm = jnp.sqrt(squared)
    factor_ref[...] = jnp.broadcast_to(limit / jnp.maximum(norm, limit), factor_ref.shape)
    for copy in sent:
        copy.wait_send()


def per_device(tokens, routes, router, w_gate, w_up, w_down, adapter, upstream, bound):
    E = lax.axis_size("expert")
    F = lax.axis_size("ffn")
    _, tl, D = tokens.shape
    t = routes.shape[1]
    FFD = w_gate.shape[2]
    cd = adapter.shape[2]
    KC = 4
    NC = max(1, min(4, D // (128 * F)))
    X, T, KW, NW = E // CORES, E * t, D // KC, D // NC
    CW = NW // F
    bf16, f32 = jnp.bfloat16, jnp.float32
    dma = pltpu.SemaphoreType.DMA
    vmem = pl.BlockSpec(memory_space=pltpu.VMEM)
    hbm = pl.BlockSpec(memory_space=pl.ANY)
    scratch = [
        pltpu.VMEM((KC, KW, FFD), bf16),
        pltpu.VMEM((KC, KW, FFD), bf16),
        pltpu.VMEM((NC, FFD, NW), bf16),
        pltpu.VMEM((D, cd), bf16),
        pltpu.VMEM((KC, E, F, tl, KW), bf16),
        pltpu.VMEM((KC, T, KW), bf16),
        pltpu.VMEM((T, FFD), f32),
        pltpu.VMEM((T, FFD), f32),
        pltpu.VMEM((T, FFD), bf16),
        pltpu.VMEM((T, E), f32),
        pltpu.VMEM((E, t, 2), jnp.int32),
        pltpu.VMEM((F, t, t), f32),
        pltpu.VMEM((NC, CORES, X, F, t, CW), bf16),
        pltpu.VMEM((NC, X, F, t, CW), bf16),
        pltpu.VMEM((NC, X, F, t, CW), bf16),
        pltpu.VMEM((NC, X, F, t, CW), bf16),
        pltpu.VMEM((NC, F, t, CW), bf16),
        pltpu.VMEM((NC, F, t, CW), bf16),
        pltpu.VMEM((NC, F, t, CW), bf16),
        dma((4, max(KC, NC))),
        dma((KC + 1,)),
        dma((E,)), dma((E,)),
        dma((F,)), dma((F,)),
        dma((KC, F)), dma((KC, F)),
        dma((KC, X)), dma((KC, X)),
        dma((KC, X)), dma((KC, X)),
        dma((NC,)), dma((NC,)),
        dma((NC, X)), dma((NC, X)),
        dma((NC, F)), dma((NC, F)),
        dma((NC, F)), dma((NC, F)),
    ]
    layer_out, adapted, factor = pl.pallas_call(
        functools.partial(layer_kernel, (E, F, KC, NC, D, FFD, t, tl, cd)),
        out_shape=(
            jax.ShapeDtypeStruct((t, D), bf16),
            jax.ShapeDtypeStruct((t, cd), bf16),
            jax.ShapeDtypeStruct((8, 128), f32),
        ),
        in_specs=[
            vmem, vmem, vmem, hbm, hbm, hbm, hbm, vmem,
            pl.BlockSpec(memory_space=pltpu.SMEM),
        ],
        out_specs=(vmem, vmem, vmem),
        scratch_shapes=scratch,
        compiler_params=pltpu.CompilerParams(
            collective_id=0, has_side_effects=True, vmem_limit_bytes=66 * 1000 * 1000
        ),
    )(
        tokens[0], routes[0], router, w_gate[0], w_up[0], w_down[0], adapter[0],
        upstream[0], bound,
    )
    adapter_grad = lax.dot_general(
        layer_out, upstream[0], (((0,), (0,)), ((), ())), preferred_element_type=jnp.float32
    )
    clipped = (adapter_grad * factor[0, 0]).astype(jnp.bfloat16)
    return (adapted[None], clipped[None])


def solution(mesh):
    in_specs = (
        P("expert", "ffn", None),
        P("expert", None, None),
        P(),
        P("expert", None, "ffn"),
        P("expert", None, "ffn"),
        P("expert", "ffn", None),
        P("expert", None, "ffn"),
        P("expert", None, "ffn"),
        P("expert"),
    )
    out_specs = (P("expert", None, "ffn"), P("expert", None, "ffn"))
    return jax.shard_map(
        per_device, mesh=mesh, in_specs=in_specs, out_specs=out_specs, check_vma=False
    )
```

time: 191 us -> 63.1 us (0.33)
  blocking collectives: 70.4 us -> 0 us
  waiting for transfers between devices: 56.4 us -> 0 us
  Pallas kernels: 0 us -> 50.5 us
  matrix products: 28 us -> 4.88 us
  between operations: 15.6 us -> 1.29 us
  starting transfers between devices: 7.03 us -> 0 us
  other arithmetic: 4.31 us -> 0 us
  local copies, waits for them, and re-layouts: 8.92 us -> 6.08 us
    pallas_call x0 -> x1, Pallas kernels: none -> 50.5 us  [per_device(): pl.pallas_call(functools.partial(layer_kernel, (E, F, KC, NC, D, FFD, t,...]
    psum x1 -> x0, blocking collectives: 37.4 us -> none  [per_device(): whole_gram = lax.psum(cotangent_gram, 'ffn')]
    psum x1 -> x0, waiting for transfers between devices: 35 us -> none  [per_device(): mixture = lax.psum(mix_share, 'ffn')]
    all_gather x1 -> x0, blocking collectives: 33 us -> none  [per_device(): gathered = lax.all_gather(tokens, 'ffn', axis=1, tiled=True)]
    dot_general x7 -> x1, matrix products: 28 us -> 4.88 us  [per_device(): lax.dot_general(layer_out, upstream[0], (((0,), (0,)), ((), ())), preferr...]
    all_to_all x2 -> x0, waiting for transfers between devices: 21.4 us -> none  [the longest x1 11.2 us: per_device(): lax.all_to_all(outgoing, 'expert', split_axis=0, concat_axis=0, tiled=True)]
    all_to_all x2 -> x0, starting transfers between devices: 6.99 us -> none  [the longest x1 3.49 us: per_device(): lax.all_to_all(outgoing, 'expert', split_axis=0, concat_axis=0, tiled=True)]
    gather x11 -> x0, local copies, waits for them, and re-layouts: 5.34 us -> none  [the longest x1 1.91 us: pack_rows(): padded[source].reshape(expert_count, capacity, token_rows.shape[1])]
  transfers between devices with their start and end apart: 3 -> 0, of which waited for: 3 -> 0; matrix products, arithmetic and copies ran while one was open for 1% -> 0% of each run, Pallas kernels for 0% -> 0%
where the time goes in v1:
time: 63.1 us; the launch traced here: 62.7 us
  Pallas kernels  50.5 us (80%)
  local copies, waits for them, and re-layouts  6.08 us (10%)
  matrix products  4.88 us (8%)
  between operations  1.29 us (2%)
    pallas_call x1, Pallas kernels, per_device(): pl.pallas_call(functools.partial(layer_kernel, (E, F, KC, NC, D, FFD, t,...  50.5 us
    dot_general x1, matrix products, per_device(): lax.dot_general(layer_out, upstream[0], (((0,), (0,)), ((), ())), preferr...  4.88 us
    unnamed x4, local copies, waits for them, and re-layouts  3.52 us
    squeeze x1, local copies, waits for them, and re-layouts, per_device(): routes[0]  1.36 us

profile of v1, /device:TPU:0, one launch (start us, length us, event | category | flops | bytes accessed | tf_op | source)
XLA Modules:
  0.0 62.7 jit_solution(7868375551322136330)
XLA Ops:
  1.3 1.4 %copy.11.routes_ref = s32[32,2]{1,0:T(8,128)} copy(s32[32,2]{0,1:T(2,128)} %bitcast.21) | data formatting | bytes 512 | tf_op jit(solution)/shard_map/squeeze | solution.py:381
  2.6 2.1 %copy.12.router_ref = bf16[4096,4]{1,0:T(8,128)(2,1)} copy(bf16[4096,4]{0,1:T(4,128)(2,1)} %param.11) | data formatting | bytes 65536 | tf_op args[2]
  4.8 0.0 copy-start
  4.8 50.5 %shard_map.104 = (bf16[32,4096]{1,0:T(8,128)(2,1)}, bf16[32,512]{1,0:T(8,128)(2,1)}, f32[8,128]{1,0:T(8,128)}) custom-call(bf16[4,4096]{1,0:T(4,128)(2,1)} %bitcast.20, s32[32,2]{1,0:T(8,128)} %copy.11.routes_ref, bf16[4096,4]{1,0:T(8,128)(2,1)} %copy.12.router_ref, bf16[4096,1536]{1,0:T(8,128)(2,1)} %bitcast.14, bf16[4096,1536]{1,0:T(8,128)(2,1)} %bitcast.15, ...), custom_call_target="tpu_custom_call" | custom-call | tf_op jit(solution)/shard_map/pallas_call | solution.py:364
  55.3 1.2 %slice.3 = f32[1,1]{1,0:T(1,128)} slice(f32[8,128]{1,0:T(8,128)} %get-tuple-element.7), slice={[0:1], [0:1]} | slice | bytes 8 | tf_op jit(solution)/shard_map/slice | solution.py:387
  56.5 0.0 copy-done
  56.5 4.9 %fusion = bf16[1,4096,512]{2,1,0:T(8,128)(2,1)} fusion(bf16[32,4096]{1,0:T(8,128)(2,1)} %get-tuple-element.6, f32[]{:T(128)} %bitcast.8, bf16[1,32,512]{2,1,0:T(8,128)(2,1)S(1)} %copy-done), kind=kOutput, calls=%fused_computation.1 | convolution fusion | flops 138412032 | bytes 4489220 | tf_op jit(solution)/shard_map/dot_general | solution.py:384
  61.4 1.4 %copy.15 = bf16[1,32,512]{2,1,0:T(8,128)(2,1)} copy(bf16[1,32,512]{2,1,0:T(8,128)(2,1)} %bitcast.19) | data formatting | bytes 65536
Async XLA Ops:
  4.8 51.7 %copy-start = (bf16[1,32,512]{2,1,0:T(8,128)(2,1)S(1)}, bf16[1,32,512]{2,1,0:T(8,128)(2,1)}, u32[]{:S(2)}) copy-start(bf16[1,32,512]{2,1,0:T(8,128)(2,1)} %param.16) | copy-start | bytes 98308

commit v2 on v1

--- a/solution.py
+++ b/solution.py
@@ -181,8 +181,9 @@
             return carry
 
         lax.fori_loop(0, FFD // FT, hidden_tile, 0)
-        part = jnp.dot(
-            tokc[k], router_ref[pl.ds(k * KW, KW), :], preferred_element_type=jnp.float32
+        part = lax.dot_general(
+            tokc[k], router_ref[:, pl.ds(k * KW, KW)], (((1,), (1,)), ((), ())),
+            preferred_element_type=jnp.float32,
         )
         logit_acc[...] = part if k == 0 else logit_acc[...] + part
 
@@ -200,10 +201,20 @@
             routes_buf.at[lax.rem(e + E - d, E)], rt_send.at[d], rt_recv.at[d],
             {"expert": lax.rem(e + d, E)},
         )
-    routed = routes_buf[...].reshape(T, 2)
+    diagonal = lax.broadcasted_iota(jnp.int32, (t, t), 0) == lax.broadcasted_iota(
+        jnp.int32, (t, t), 1
+    )
+
+    def choice(k):
+        named = [routes_buf[c][k:k + 1, :].astype(jnp.float32) for c in range(E)]
+        return jnp.concatenate(
+            [jnp.sum(jnp.where(diagonal, row, 0.0), axis=1, keepdims=True) for row in named],
+            axis=0,
+        ).astype(jnp.int32)
+
+    first, second = choice(0), choice(1)
     logits = logit_acc[...]
     expert_ids = lax.broadcasted_iota(jnp.int32, (T, E), 1)
-    first, second = routed[:, 0:1], routed[:, 1:2]
     picked_first = jnp.sum(jnp.where(expert_ids == first, logits, 0.0), axis=1, keepdims=True)
     picked_second = jnp.sum(jnp.where(expert_ids == second, logits, 0.0), axis=1, keepdims=True)
     weight_first = 1.0 / (1.0 + jnp.exp(picked_second - picked_first))
@@ -312,6 +323,27 @@
     factor_ref[...] = jnp.broadcast_to(limit / jnp.maximum(norm, limit), factor_ref.shape)
     for copy in sent:
         copy.wait_send()
+
+
+def grad_kernel(
+    RB, layer_ref, up_ref, factor_ref, adapted_in, adapted_ref, clipped_hbm, blocks, sems
+):
+    factor = factor_ref[0:1, 0:1]
+    copies = []
+    for i in range(blocks.shape[0]):
+        grad = lax.dot_general(
+            layer_ref[:, i * RB:(i + 1) * RB], up_ref[...], (((0,), (0,)), ((), ())),
+            preferred_element_type=jnp.float32,
+        )
+        blocks[i] = (grad * factor).astype(jnp.bfloat16)
+        copy = pltpu.make_async_copy(
+            blocks.at[i], clipped_hbm.at[pl.ds(i * RB, RB), :], sems.at[i]
+        )
+        copy.start()
+        copies.append(copy)
+    adapted_ref[...] = adapted_in[...]
+    for copy in copies:
+        copy.wait()
 
 
 def per_device(tokens, routes, router, w_gate, w_up, w_down, adapter, upstream, bound):
@@ -340,7 +372,7 @@
         pltpu.VMEM((T, FFD), f32),
         pltpu.VMEM((T, FFD), bf16),
         pltpu.VMEM((T, E), f32),
-        pltpu.VMEM((E, t, 2), jnp.int32),
+        pltpu.VMEM((E, 2, t), jnp.int32),
         pltpu.VMEM((F, t, t), f32),
         pltpu.VMEM((NC, CORES, X, F, t, CW), bf16),
         pltpu.VMEM((NC, X, F, t, CW), bf16),
@@ -375,16 +407,23 @@
         out_specs=(vmem, vmem, vmem),
         scratch_shapes=scratch,
         compiler_params=pltpu.CompilerParams(
-            collective_id=0, has_side_effects=True, vmem_limit_bytes=66 * 1000 * 1000
+            collective_id=0, has_side_effects=True, vmem_limit_bytes=63_500_000
         ),
     )(
-        tokens[0], routes[0], router, w_gate[0], w_up[0], w_down[0], adapter[0],
+        tokens[0], routes[0].T, router.T, w_gate[0], w_up[0], w_down[0], adapter[0],
         upstream[0], bound,
     )
-    adapter_grad = lax.dot_general(
-        layer_out, upstream[0], (((0,), (0,)), ((), ())), preferred_element_type=jnp.float32
-    )
-    clipped = (adapter_grad * factor[0, 0]).astype(jnp.bfloat16)
+    RB = D // 8
+    adapted, clipped = pl.pallas_call(
+        functools.partial(grad_kernel, RB),
+        out_shape=(
+            jax.ShapeDtypeStruct((t, cd), bf16),
+            jax.ShapeDtypeStruct((D, cd), bf16),
+        ),
+        in_specs=[vmem, vmem, vmem, vmem],
+        out_specs=(vmem, hbm),
+        scratch_shapes=[pltpu.VMEM((D // RB, RB, cd), bf16), dma((D // RB,))],
+    )(layer_out, upstream[0], factor, adapted)
     return (adapted[None], clipped[None])
 
 

time: 63.1 us -> 55.5 us (0.88)
  local copies, waits for them, and re-layouts: 6.08 us -> 0 us
  matrix products: 4.88 us -> 0 us
  Pallas kernels: 50.5 us -> 54 us
    dot_general x1 -> x0, matrix products: 4.88 us -> none  [per_device(): lax.dot_general(layer_out, upstream[0], (((0,), (0,)), ((), ())), preferr...]
    pallas_call x0 -> x1, Pallas kernels: none -> 3.99 us  [per_device(): pl.pallas_call(functools.partial(grad_kernel, RB), out_shape=(jax.ShapeDt...]
    unnamed x4 -> x0, local copies, waits for them, and re-layouts: 3.52 us -> none
    squeeze x1 -> x0, local copies, waits for them, and re-layouts: 1.36 us -> none  [per_device(): routes[0]]
    slice x1 -> x0, local copies, waits for them, and re-layouts: 1.19 us -> none  [per_device(): clipped = (adapter_grad * factor[0, 0]).astype(jnp.bfloat16)]
where the time goes in v2:
time: 55.5 us; the launch traced here: 55.3 us
  Pallas kernels  54 us (97%)
  between operations  1.29 us (2%)
    pallas_call x1, Pallas kernels, per_device(): pl.pallas_call(functools.partial(layer_kernel, (E, F, KC, NC, D, FFD, t,...  50 us
    pallas_call x1, Pallas kernels, per_device(): pl.pallas_call(functools.partial(grad_kernel, RB), out_shape=(jax.ShapeDt...  3.99 us

profile of v2, /device:TPU:0, one launch (start us, length us, event | category | flops | bytes accessed | tf_op | source)
XLA Modules:
  0.0 55.3 jit_solution(5213420538747557329)
XLA Ops:
  1.3 50.0 %shard_map.104 = (bf16[32,4096]{1,0:T(8,128)(2,1)}, bf16[32,512]{1,0:T(8,128)(2,1)}, f32[8,128]{1,0:T(8,128)}) custom-call(bf16[4,4096]{1,0:T(4,128)(2,1)} %bitcast.18, s32[2,32]{1,0:T(2,128)} %bitcast.20, bf16[4,4096]{1,0:T(4,128)(2,1)} %bitcast.19, bf16[4096,1536]{1,0:T(8,128)(2,1)} %bitcast.12, bf16[4096,1536]{1,0:T(8,128)(2,1)} %bitcast.13, ...), custom_call_target="tpu_custom_call" | custom-call | tf_op jit(solution)/shard_map/pallas_call | solution.py:396
  51.3 4.0 %shard_map.105 = (bf16[32,512]{1,0:T(8,128)(2,1)}, bf16[4096,512]{1,0:T(8,128)(2,1)}) custom-call(bf16[32,4096]{1,0:T(8,128)(2,1)} %get-tuple-element.7.layer_ref, bf16[32,512]{1,0:T(8,128)(2,1)} %bitcast.17, f32[8,128]{1,0:T(8,128)} %get-tuple-element.8.factor_ref, bf16[32,512]{1,0:T(8,128)(2,1)} %get-tuple-element.9.adapted_in), custom_call_target="tpu_custom_call" | custom-call | tf_op jit(solution)/shard_map/pallas_call | solution.py:417
